TPU v7x, 128 devices: a whole 4x4x4 slice. The times are simulated.
128 devices in a mesh: dp: 8 (over z, core), expert: 16 (over y, x).
Axes of the slice: x: 4, y: 4, z: 4, core: 2. Of those that a mesh axis runs over, the one named last changes fastest.
Arguments:
- tokens: bfloat16 [131072, 2080], P(('dp', 'expert')), may hold values from -6 to 6
- router_logits: bfloat16 [131072, 2048], P(('dp', 'expert')), may hold values from -300 to 300
- gate_grad: float32 [131072], P(('dp', 'expert')), may hold values from -6 to 6
- expert_index: int32 [131072, 1], P(('dp', 'expert')), may hold values from 0 to 2047
- keep_mask: int32 [2048], replicated, may hold values 0 or 1
Outputs:
- router_grad: float32 [2048, 2080], P('expert', 'dp')
All inputs are finite; a program needn't handle non-finite values.
Results may differ from a plain program's by a relative error of at most 0.0003.
Values sent between devices are 32-bit elements; how exact they have to be, the bound alone decides.
A program may use at most 128 MiB of HBM per device.

v0:
```python
import math

import jax
import jax.numpy as jnp
from jax import lax
from jax.sharding import Mesh
from jax.sharding import PartitionSpec as P

DP = ("dp_0", "dp_1")
EXPERT = ("expert_0", "expert_1")
DP_EXPERT = ("dp_0", "dp_1", "expert_0", "expert_1")


def over_axes(value, axes):
    for axis in axes:
        value = lax.psum(value, axis)
    return value


def in_blocks(value, dim, devices):
    before, after = (value.shape[:dim], value.shape[dim + 1 :])
    return jnp.moveaxis(value.reshape(*before, devices, -1, *after), dim, 0)


def sent_and_summed(value, axis, dim):
    devices = lax.axis_size(axis)
    tiles = lax.all_to_all(in_blocks(value, dim, devices), axis, 0, 0, tiled=True)
    return jnp.sum(tiles, axis=0)


def make_term(grad_source, wide_tokens):
    return lax.dot_general(
        grad_source,
        wide_tokens,
        (((0,), (0,)), ((), ())),
        precision=lax.Precision.HIGHEST,
        preferred_element_type=jnp.float32,
    )


def local(tokens, router_logits, gate_grad, expert_index, keep_mask):
    tok_rows = tokens.shape[0]
    expert_total = router_logits.shape[1]
    dp_width = lax.axis_size(DP)
    expert_width = lax.axis_size(EXPERT)
    total_tokens = tok_rows * dp_width * expert_width
    block_rows = math.gcd(tok_rows, 512)
    block_count = tok_rows // block_rows
    routed = expert_index[:, 0].reshape(block_count, block_rows)
    logit_blocks = router_logits.reshape(block_count, block_rows, expert_total)
    gate_blocks = gate_grad.reshape(block_count, block_rows)

    def block_counts(routed_block):
        columns = lax.broadcasted_iota(jnp.int32, (block_rows, expert_total), 1)
        return jnp.sum((columns == routed_block[:, None]).astype(jnp.int32), axis=0)

    local_counts = jnp.sum(lax.map(block_counts, routed), axis=0)
    counts = over_axes(local_counts, DP_EXPERT)
    aux_cost = counts.astype(jnp.float32) * (expert_total / total_tokens)
    kept_cols = keep_mask.astype(jnp.float32)

    def block_grad(inputs):
        logit_block, gate_block, routed_block = inputs
        scores = logit_block.astype(jnp.float32)
        row_peak = jnp.max(scores, axis=1, keepdims=True)
        weights = jnp.exp(scores - row_peak)
        router_probs = weights / jnp.sum(weights, axis=1, keepdims=True)
        columns = lax.broadcasted_iota(jnp.int32, scores.shape, 1)
        chosen = columns == routed_block[:, None]
        top_prob = jnp.sum(jnp.where(chosen, router_probs, 0.0), axis=1)
        spread = jnp.dot(router_probs, aux_cost, precision=lax.Precision.HIGHEST)
        gate_part = (gate_block * top_prob)[:, None] * (chosen.astype(jnp.float32) - router_probs)
        aux_part = router_probs * (aux_cost[None, :] - spread[:, None])
        return kept_cols[None, :] * (gate_part + aux_part)

    logit_grad = lax.map(block_grad, (logit_blocks, gate_blocks, routed)).reshape(
        tok_rows, expert_total
    )
    wide_tokens = tokens.astype(jnp.float32)
    owned = lax.psum_scatter(
        make_term(logit_grad, wide_tokens), EXPERT, scatter_dimension=0, tiled=True
    )
    result = sent_and_summed(owned, DP, 1)
    return result


def solution(mesh):
    split = Mesh(mesh.devices.reshape(4, 2, 4, 4), ("dp_0", "dp_1", "expert_0", "expert_1"))
    in_specs = (P(DP_EXPERT, None), P(DP_EXPERT, None), P(DP_EXPERT), P(DP_EXPERT, None), P())
    out_specs = P(EXPERT, DP)
    return jax.shard_map(local, mesh=split, in_specs=in_specs, out_specs=out_specs, check_vma=False)
```

profile of v0, /device:TPU:0, one launch (start us, length us, event | category | flops | bytes accessed | tf_op | source)
XLA Modules:
  0.0 244.3 jit_solution(4860561049310247825)
XLA Ops:
  6.5 0.5 broadcast.96
  7.0 1.3 reduce.8
  8.3 0.7 reshape.141
  9.0 0.7 convert_element_type.38
  9.7 1.4 while.22
  9.7 0.6 convert_reduce_fusion.2
  10.3 0.1 dynamic_update_slice.14
  10.4 0.6 convert_reduce_fusion.2
  11.0 0.1 dynamic_update_slice.14
  11.1 10.0 %psum.28 = s32[2048]{0:T(1024)S(1)} all-reduce(s32[2048]{0:T(1024)S(1)} %reduce_sum.51), channel_id=1, replica_groups=mesh['dp_0'=4,'dp_1'=2,'expert_0'=4,'expert_1'=4] {'dp_0'}, use_global_device_ids=true, to_apply=%region_4.5 | all-reduce | flops 2048 | bytes 16384 | tf_op jit(solution)/shard_map/psum | solution.py:16
  21.1 1.8 psum.29
  22.9 9.2 %psum.30 = s32[2048]{0:T(1024)S(1)} all-reduce(s32[2048]{0:T(1024)S(1)} %psum.29), channel_id=1, replica_groups=mesh['dp_0'=4,'dp_1'=2,'expert_0'=4,'expert_1'=4] {'expert_0'}, use_global_device_ids=true, to_apply=%region_6.7 | all-reduce | flops 2048 | bytes 16384 | tf_op jit(solution)/shard_map/psum | solution.py:16
  32.1 9.0 %psum.31 = s32[2048]{0:T(1024)S(1)} all-reduce(s32[2048]{0:T(1024)S(1)} %psum.30), channel_id=1, replica_groups=mesh['dp_0'=4,'dp_1'=2,'expert_0'=4,'expert_1'=4] {'expert_1'}, use_global_device_ids=true, to_apply=%region_7.8 | all-reduce | flops 2048 | bytes 16384 | tf_op jit(solution)/shard_map/psum | solution.py:16
  41.1 33.4 %while.23 = (s32[]{:T(128)}, f32[2,512,2048]{2,1,0:T(8,128)}, f32[2048]{0:T(1024)S(1)}, f32[2,512]{1,0:T(2,128)S(1)}, s32[2,512]{1,0:T(2,128)S(1)}, /*index=5*/b...) while((s32[]{:T(128)}, f32[2,512,2048]{2,1,0:T(8,128)}, f32[2048]{0:T(1024)S(1)}, ...), condition=%wide.region_12.13_spmd, body=%wide.region_8.12_spmd.sunk | while | flops 37748224 | bytes 90249440 | solution.py:76
  41.1 2.1 dynamic-slice_reduce_fusion.2
  43.2 2.6 %fusion.22 = f32[512]{0:T(512)S(1)} fusion(f32[512]{0:T(512)S(1)} %reduce_max.18, bf16[2,512,2048]{2,1,0:T(8,128)(2,1)} %get-tuple-element.231, s32[]{:T(128)S(6)} %copy.16), kind=kLoop, calls=%fused_computation.8.clone.1 | loop fusion | flops 3145216 | bytes 2101252 | tf_op jit(solution)/shard_map/while/body/eval_jaxpr/reduce_sum | solution.py:67
  45.8 4.4 %fusion.23 = f32[1,512]{1,0:T(1,128)S(1)} fusion(f32[2048,1]{0,1:T(1,128)S(1)} %bitcast.52, f32[512]{0:T(512)S(1)} %fusion.22, f32[512]{0:T(512)S(1)} %reduce_max.18, bf16[2,512,2048]{2,1,0:T(8,128)(2,1)S(1)} %copy-done, s32[]{:T(128)S(6)} %copy.16), kind=kOutput, calls=%fused_computation.15.clone.1 | convolution fusion | flops 15728640 | bytes 2111492 | tf_op jit(solution)/shard_map/while/body/eval_jaxpr/dot_general | solution.py:71
  50.2 1.7 select_reduce_fusion.2
  52.0 2.6 %multiply_dynamic-update-slice_fusion.2 = f32[2,512,2048]{2,1,0:T(8,128)S(1)} fusion(f32[2,512,2048]{2,1,0:T(8,128)S(1)} %bitcast.58, s32[]{:T(128)S(6)} %copy.16, f32[512]{0:T(512)S(1)} %bitcast.55, f32[2048]{0:T(1024)S(1)} %get-tuple-element.232, f32[512]{0:T(512)S(1)} %fusion.22, f32[512]{0:T(512)S(1)} %reduce_max.18, s32[512]{0:T(512)S(1)} %bitcast.51, ...), kind=kLoop, calls=%fused_computation.11.clone.1 | loop fusion | flops 11534336 | bytes 6318084 | tf_op jit(solution)/shard_map/while/body/jit(dynamic_update_index_in_dim)/dynamic_update_slice | solution.py:76
  54.6 3.2 %copy-done.1 = f32[2,512,2048]{2,1,0:T(8,128)} copy-done((f32[2,512,2048]{2,1,0:T(8,128)}, f32[2,512,2048]{2,1,0:T(8,128)S(1)}, u32[]{:S(2)}) %copy-start.1) | copy-done | bytes 8388632 | tf_op jit(solution)/shard_map/while
  57.8 2.1 dynamic-slice_reduce_fusion.2
  59.9 2.6 %fusion.22 = f32[512]{0:T(512)S(1)} fusion(f32[512]{0:T(512)S(1)} %reduce_max.18, bf16[2,512,2048]{2,1,0:T(8,128)(2,1)} %get-tuple-element.231, s32[]{:T(128)S(6)} %copy.16), kind=kLoop, calls=%fused_computation.8.clone.1 | loop fusion | flops 3145216 | bytes 2101252 | tf_op jit(solution)/shard_map/while/body/eval_jaxpr/reduce_sum | solution.py:67
  62.5 4.4 %fusion.23 = f32[1,512]{1,0:T(1,128)S(1)} fusion(f32[2048,1]{0,1:T(1,128)S(1)} %bitcast.52, f32[512]{0:T(512)S(1)} %fusion.22, f32[512]{0:T(512)S(1)} %reduce_max.18, bf16[2,512,2048]{2,1,0:T(8,128)(2,1)S(1)} %copy-done, s32[]{:T(128)S(6)} %copy.16), kind=kOutput, calls=%fused_computation.15.clone.1 | convolution fusion | flops 15728640 | bytes 2111492 | tf_op jit(solution)/shard_map/while/body/eval_jaxpr/dot_general | solution.py:71
  66.9 1.7 select_reduce_fusion.2
  68.7 2.6 %multiply_dynamic-update-slice_fusion.2 = f32[2,512,2048]{2,1,0:T(8,128)S(1)} fusion(f32[2,512,2048]{2,1,0:T(8,128)S(1)} %bitcast.58, s32[]{:T(128)S(6)} %copy.16, f32[512]{0:T(512)S(1)} %bitcast.55, f32[2048]{0:T(1024)S(1)} %get-tuple-element.232, f32[512]{0:T(512)S(1)} %fusion.22, f32[512]{0:T(512)S(1)} %reduce_max.18, s32[512]{0:T(512)S(1)} %bitcast.51, ...), kind=kLoop, calls=%fused_computation.11.clone.1 | loop fusion | flops 11534336 | bytes 6318084 | tf_op jit(solution)/shard_map/while/body/jit(dynamic_update_index_in_dim)/dynamic_update_slice | solution.py:76
  71.3 3.2 %copy-done.1 = f32[2,512,2048]{2,1,0:T(8,128)} copy-done((f32[2,512,2048]{2,1,0:T(8,128)}, f32[2,512,2048]{2,1,0:T(8,128)S(1)}, u32[]{:S(2)}) %copy-start.1) | copy-done | bytes 8388632 | tf_op jit(solution)/shard_map/while
  74.5 32.6 %fusion.12 = f32[2048,2080]{0,1:T(8,128)} fusion(f32[1024,2048]{1,0:T(8,128)} %bitcast.59, bf16[1024,2080]{0,1:T(8,128)(2,1)} %param.9), kind=kOutput, calls=%fused_computation.24 | convolution fusion | flops 52344913920 | bytes 29687808 | tf_op jit(solution)/shard_map/dot_general | solution.py:32
  107.2 0.0 reduce-scatter.2.cloned.1.call-update
  107.2 107.6 %reduce-scatter.2.cloned.1.call-done = f32[128,2080]{0,1:T(8,128)} async-done(((f32[2048,2080]{0,1:T(8,128)}), f32[128,2080]{0,1:T(8,128)}) %reduce-scatter.2.cloned.1.call-update) | async-done | bytes 1064976 | tf_op jit(solution)/shard_map/reduce_scatter | solution.py:80
  214.8 1.3 reshape.144
  216.1 20.6 %all_to_all.5 = f32[8,128,260]{1,2,0:T(8,128)S(1)} all-to-all(f32[8,128,260]{1,2,0:T(8,128)S(1)} %bitcast.49), channel_id=1, replica_groups=mesh['dp_0'=4,'dp_1'=2,'expert_0'=4,'expert_1'=4] {'dp_0','dp_1'}, dimensions={0} | all-to-all | bytes 2129920 | tf_op jit(solution)/shard_map/all_to_all | solution.py:27
  236.7 0.7 reduce_sum.52
  (32 shorter events, 0.1 us)
Async XLA Ops:
  6.5 208.3 %reduce-scatter.2.cloned.1.call-start = ((), (), s32[]{:S(2)}) async-start(), calls=%async_computation.2 | async-start | bytes 18104320 | tf_op jit(solution)/shard_map/reduce_scatter | solution.py:80
  41.1 4.7 %copy-start = (bf16[2,512,2048]{2,1,0:T(8,128)(2,1)S(1)}, bf16[2,512,2048]{2,1,0:T(8,128)(2,1)}, u32[]{:S(2)}) copy-start(bf16[2,512,2048]{2,1,0:T(8,128)(2,1)} %get-tuple-element.231) | copy-start | bytes 12582916 | tf_op jit(solution)/shard_map/while
  43.2 8.7 %slice-start = ((s8[8388608]{0:T(1024)(128)(4,1)}), s8[4194304]{0:T(1024)(128)(4,1)S(1)}, s32[]{:S(2)}) async-start(s8[8388608]{0:T(1024)(128)(4,1)} %bitcast.57), calls=%async_computation.3 | async-start | bytes 8388608 | tf_op jit(solution)/shard_map/while
  45.8 6.1 %slice-start.1 = ((s8[8388608]{0:T(1024)(128)(4,1)}), s8[4194304]{0:T(1024)(128)(4,1)S(1)}, s32[]{:S(2)}) async-start(s8[8388608]{0:T(1024)(128)(4,1)} %bitcast.57), calls=%async_computation.4 | async-start | bytes 8388608 | tf_op jit(solution)/shard_map/while
  54.6 3.2 %copy-start.1 = (f32[2,512,2048]{2,1,0:T(8,128)}, f32[2,512,2048]{2,1,0:T(8,128)S(1)}, u32[]{:S(2)}) copy-start(f32[2,512,2048]{2,1,0:T(8,128)S(1)} %multiply_dynamic-update-slice_fusion.2) | copy-start | bytes 25165828 | tf_op jit(solution)/shard_map/while
  57.8 4.7 %copy-start = (bf16[2,512,2048]{2,1,0:T(8,128)(2,1)S(1)}, bf16[2,512,2048]{2,1,0:T(8,128)(2,1)}, u32[]{:S(2)}) copy-start(bf16[2,512,2048]{2,1,0:T(8,128)(2,1)} %get-tuple-element.231) | copy-start | bytes 12582916 | tf_op jit(solution)/shard_map/while
  59.9 8.7 %slice-start = ((s8[8388608]{0:T(1024)(128)(4,1)}), s8[4194304]{0:T(1024)(128)(4,1)S(1)}, s32[]{:S(2)}) async-start(s8[8388608]{0:T(1024)(128)(4,1)} %bitcast.57), calls=%async_computation.3 | async-start | bytes 8388608 | tf_op jit(solution)/shard_map/while
  62.5 6.1 %slice-start.1 = ((s8[8388608]{0:T(1024)(128)(4,1)}), s8[4194304]{0:T(1024)(128)(4,1)S(1)}, s32[]{:S(2)}) async-start(s8[8388608]{0:T(1024)(128)(4,1)} %bitcast.57), calls=%async_computation.4 | async-start | bytes 8388608 | tf_op jit(solution)/shard_map/while
  71.3 3.2 %copy-start.1 = (f32[2,512,2048]{2,1,0:T(8,128)}, f32[2,512,2048]{2,1,0:T(8,128)S(1)}, u32[]{:S(2)}) copy-start(f32[2,512,2048]{2,1,0:T(8,128)S(1)} %multiply_dynamic-update-slice_fusion.2) | copy-start | bytes 25165828 | tf_op jit(solution)/shard_map/while
Sparse Core Ops, SparseCore 0:
  107.3 107.4 reduce-scatter.1
where the time goes:
time: 245 us; the launch traced here: 244 us
  waiting for transfers between devices  108 us (44%)
  blocking collectives  50.6 us (21%)
  matrix products  41.4 us (17%)
  other arithmetic  21.9 us (9%)
  between operations  13.4 us (5%)
  local copies, waits for them, and re-layouts  9.18 us (4%)
    reduce_scatter x1, waiting for transfers between devices, local(): lax.psum_scatter(make_term(logit_grad, wide_tokens), EXPERT, scatter_dime...  108 us
    dot_general x1, matrix products, make_term(): lax.dot_general(grad_source, wide_tokens, (((0,), (0,)), ((), ())), preci...  32.6 us
    psum x4, blocking collectives, over_axes(): value = lax.psum(value, axis)  30 us
    all_to_all x1, blocking collectives, sent_and_summed(): lax.all_to_all(in_blocks(value, dim, devices), axis, 0, 0, tiled=True)  20.6 us
    dot_general x2, matrix products, block_grad(): spread = jnp.dot(router_probs, aux_cost, precision=lax.Precision.HIGHEST)  8.72 us
    while x16, local copies, waits for them, and re-layouts  6.45 us
    dynamic_update_slice x2, other arithmetic, local(): lax.map(block_grad, (logit_blocks, gate_blocks, routed))  5.28 us
    reduce_sum x2, other arithmetic, block_grad(): router_probs = weights / jnp.sum(weights, axis=1, keepdims=True)  5.13 us
  transfers between devices with their start and end apart: 1, of which 1 were waited for; matrix products, arithmetic and copies ran while one was open for 0% of the time, Pallas kernels for 0%

commit v1 on v0

v1 whole, which is shorter than its diff:
```python
import functools

import jax
import jax.numpy as jnp
from jax import lax
from jax.experimental import pallas as pl
from jax.experimental.pallas import tpu as pltpu
from jax.sharding import PartitionSpec as P

MESH = pl.DeviceIdType.MESH
RING = 4
LANES = 128
ROW_CHUNKS = (8, 16, 16, 16, 16, 16)
TB = 128


def kernel(total_tokens, idx_ref, gate_ref, keep_ref, tok_ref, logit_ref, out_ref,
           lbuf, xbuf, icol, acol, invc, ptab, gmat, xf, xt, cbuf, drecv, sums, r1m, r1f, tmid, r2, umid, r3,
           fin, cnt, cnt_recv, aux_ref,
           lsem, xsem, csend, crecv, dsend, drsem, ssem, rsem):
    tok_rows, d_model = tok_ref.shape
    experts = logit_ref.shape[1]
    eblocks = experts // LANES
    blocks = tok_rows // TB
    chunks = len(ROW_CHUNKS)
    offsets = [sum(ROW_CHUNKS[:k]) for k in range(chunks)]

    dp = lax.axis_index("dp")
    ex = lax.axis_index("expert")
    zc, core = dp // 2, dp % 2
    yc, xc = ex // RING, ex % RING
    here = {"x": xc, "y": yc, "z": zc}

    def device(**moved):
        at = dict(here, **moved)
        return (2 * at["z"] + core, RING * at["y"] + at["x"])

    sibling = (2 * zc + 1 - core, ex)

    def away(axis, step):
        return device(**{axis: (here[axis] + step) % RING})

    def load_logits(b, slot):
        return pltpu.make_async_copy(logit_ref.at[pl.ds(b * TB, TB), :], lbuf.at[slot], lsem.at[slot])

    def load_tokens(b, slot):
        return pltpu.make_async_copy(tok_ref.at[pl.ds(b * TB, TB), :], xbuf.at[slot], xsem.at[slot])

    load_logits(0, 0).start()
    load_logits(1, 1).start()
    load_tokens(0, 0).start()
    load_tokens(1, 1).start()

    barrier = pltpu.get_barrier_semaphore()
    peers = [sibling] + [away(axis, step) for axis in "xyz" for step in (1, 2, 3)]
    for peer in peers:
        pl.semaphore_signal(barrier, inc=1, device_id=peer, device_id_type=MESH)

    idx = idx_ref[...]
    total = jnp.zeros((eblocks, LANES), jnp.float32)
    for b in range(blocks):
        row = idx[b : b + 1, :]
        high = (row // LANES == lax.broadcasted_iota(jnp.int32, (eblocks, LANES), 0)).astype(jnp.bfloat16)
        low = (row % LANES == lax.broadcasted_iota(jnp.int32, (LANES, LANES), 0)).astype(jnp.bfloat16)
        total = total + lax.dot_general(high, low, (((1,), (1,)), ((), ())), preferred_element_type=jnp.float32)
    cnt[0] = total.astype(jnp.int32)

    pl.semaphore_wait(barrier, len(peers))

    def count_copies(stage):
        if stage == 0:
            return [pltpu.make_async_remote_copy(cnt.at[0], cnt_recv.at[0], csend.at[0], crecv.at[0], device_id=sibling, device_id_type=MESH)]
        axis = "xyz"[stage - 1]
        copies = []
        for step in (1, 2, 3):
            slot = 1 + 3 * (stage - 1) + step - 1
            copies.append(pltpu.make_async_remote_copy(
                cnt.at[stage], cnt_recv.at[slot], csend.at[slot], crecv.at[slot], device_id=away(axis, step), device_id_type=MESH))
        return copies

    def count_arrive(stage):
        value = cnt[stage]
        for number, copy in enumerate(count_copies(stage)):
            copy.wait_recv()
            slot = 0 if stage == 0 else 1 + 3 * (stage - 1) + number
            value = value + cnt_recv[slot]
        return value

    def count_step(stage):
        cnt[stage + 1] = count_arrive(stage)
        for copy in count_copies(stage + 1):
            copy.start()

    for copy in count_copies(0):
        copy.start()

    idx_t = jnp.transpose(idx.astype(jnp.float32))
    gate_t = jnp.transpose(gate_ref[...])
    for b in range(blocks):
        icol[b * TB : (b + 1) * TB, :] = jnp.broadcast_to(idx_t[:, b : b + 1], (TB, LANES)).astype(jnp.int32)
        acol[b * TB : (b + 1) * TB, :] = jnp.broadcast_to(gate_t[:, b : b + 1], (TB, LANES))

    RS = 32

    def lane_of(j):
        return lax.broadcasted_iota(jnp.int32, (RS, LANES), 1) + j * LANES

    def stats_block(b):
        slot = b % 2
        load_logits(b, slot).wait()

        def rows(r, carry):
            local = pl.ds(pl.multiple_of(r * RS, RS), RS)
            at = pl.ds(pl.multiple_of(b * TB + r * RS, RS), RS)
            peak = lbuf[slot, local, 0:LANES].astype(jnp.float32)
            for j in range(1, eblocks):
                peak = jnp.maximum(peak, lbuf[slot, local, j * LANES : (j + 1) * LANES].astype(jnp.float32))
            peak = jnp.max(peak, axis=1, keepdims=True)
            mass = jnp.zeros((RS, LANES), jnp.float32)
            top = jnp.zeros((RS, LANES), jnp.float32)
            chosen = icol[at, :]
            for j in range(eblocks):
                weight = jnp.exp(lbuf[slot, local, j * LANES : (j + 1) * LANES].astype(jnp.float32) - peak)
                ptab[at, j * LANES : (j + 1) * LANES] = weight
                mass = mass + weight
                top = top + jnp.where(chosen == lane_of(j), weight, 0.0)
            inverse = 1.0 / jnp.sum(mass, axis=1, keepdims=True)
            top_prob = jnp.sum(top, axis=1, keepdims=True) * inverse
            invc[at, :] = jnp.broadcast_to(inverse, (RS, LANES))
            acol[at, :] = acol[at, :] * top_prob
            return carry

        lax.fori_loop(0, TB // RS, rows, 0)

    def xpose_block(b):
        slot = b % 2
        load_tokens(b, slot).wait()
        for c in range(0, d_model, LANES):
            width = min(LANES, d_model - c)
            xf[c : c + width, :] = jnp.transpose(xbuf[slot, :, c : c + width].astype(jnp.float32))
        cols = pl.ds(pl.multiple_of(b * TB, TB), TB)
        for k in range(chunks):
            r = ROW_CHUNKS[k]
            pieces = []
            for group in range(24):
                cc, zz, part = group // 12, (group // 3) % 4, group % 3
                src = (d_model // RING) * zz + 256 * cc + 88 * part + offsets[k]
                pieces.append(xf[src : src + r, :])
            dst = 24 * offsets[k]
            if r == 8:
                for g in range(0, 24, 2):
                    xt[dst + 8 * g : dst + 8 * g + 16, cols] = jnp.concatenate([pieces[g], pieces[g + 1]], axis=0).astype(jnp.bfloat16)
            else:
                for g in range(24):
                    xt[dst + r * g : dst + r * (g + 1), cols] = pieces[g].astype(jnp.bfloat16)

    def prep(b, carry):
        stats_block(b)

        @pl.when(b + 2 < blocks)
        def _():
            load_logits(b + 2, b % 2).start()

        xpose_block(b)

        @pl.when(b + 2 < blocks)
        def _():
            load_tokens(b + 2, b % 2).start()

        return carry

    lax.fori_loop(0, 2, prep, 0)
    count_step(0)
    lax.fori_loop(2, 4, prep, 0)
    count_step(1)
    lax.fori_loop(4, 7, prep, 0)
    count_step(2)
    lax.fori_loop(7, 8, prep, 0)

    aux_ref[...] = count_arrive(3).astype(jnp.float32) * (experts / total_tokens)
    aux = aux_ref[...]

    def grad_rows(r, carry):
        at = pl.ds(pl.multiple_of(r * RS, RS), RS)
        acc = ptab[at, 0:LANES] * aux[0:1, :]
        for j in range(1, eblocks):
            acc = acc + ptab[at, j * LANES : (j + 1) * LANES] * aux[j : j + 1, :]
        inverse = invc[at, :]
        spread = jnp.sum(acc, axis=1, keepdims=True) * inverse
        gain = acol[at, :]
        drop = spread + gain
        chosen = icol[at, :]
        for j in range(eblocks):
            value = (ptab[at, j * LANES : (j + 1) * LANES] * inverse) * (aux[j : j + 1, :] - drop)
            value = value + jnp.where(chosen == lane_of(j), gain, 0.0)
            big = value.astype(jnp.bfloat16)
            gmat[0, at, j * LANES : (j + 1) * LANES] = big
            gmat[1, at, j * LANES : (j + 1) * LANES] = (value - big.astype(jnp.float32)).astype(jnp.bfloat16)
        return carry

    lax.fori_loop(0, tok_rows // RS, grad_rows, 0)

    NT = 256

    def pair_copy(k):
        rows = 12 * ROW_CHUNKS[k]
        src = cbuf.at[k % 2, :, pl.ds(pl.multiple_of((1 - core) * rows, 8), rows), :]
        return pltpu.make_async_remote_copy(src, drecv[k], dsend.at[k], drsem.at[k], device_id=sibling, device_id_type=MESH)

    def matmul_chunk(k):
        if k >= 2:
            pair_copy(k - 2).wait_send()
        rows = 24 * ROW_CHUNKS[k]
        base = 24 * offsets[k]

        def tile(n, carry):
            cols = pl.ds(pl.multiple_of(n * NT, NT), NT)
            left = xt[base : base + rows, :]
            value = jnp.dot(left, gmat[0, :, cols], preferred_element_type=jnp.float32)
            value = value + jnp.dot(left, gmat[1, :, cols], preferred_element_type=jnp.float32)
            for half in range(NT // LANES):
                cbuf[k % 2, n * (NT // LANES) + half, 0:rows, :] = value[:, half * LANES : (half + 1) * LANES]
            return carry

        lax.fori_loop(0, experts // NT, tile, 0)
        pair_copy(k).start()

    orders = ("xyz", "yzx", "zxy")

    def rcopy(k, p, n, src, dst, peer):
        return pltpu.make_async_remote_copy(src, dst, ssem.at[k, p, n], rsem.at[k, p, n], device_id=peer, device_id_type=MESH)

    def pos(p, stage):
        return here[orders[p][stage]]

    def ring1(k, p, numbers):
        axis = orders[p][0]
        i = pos(p, 0)
        up, down, far = (i + 1) % RING, (i + 3) % RING, (i + 2) % RING
        right, left = away(axis, 1), away(axis, 3)
        s, m, f = sums[k], r1m[k], r1f[k]
        table = (
            (s.at[p, far, 0:2], m.at[p, 0], right),
            (s.at[p, far, 2:4], m.at[p, 1], left),
            (s.at[p, up, 2:4], f.at[p, 0, 2:4], right),
            (s.at[p, down, 0:2], f.at[p, 1, 0:2], left),
            (s.at[p, up, 0:2], f.at[p, 0, 0:2], right),
            (s.at[p, down, 2:4], f.at[p, 1, 2:4], left),
        )
        return [rcopy(k, p, n, *table[n]) for n in numbers]

    def ring2(k, p):
        axis, i = orders[p][1], pos(p, 1)
        return [rcopy(k, p, 5 + step, tmid[k].at[p, (i + step) % RING], r2[k].at[p, step - 1], away(axis, step)) for step in (1, 2, 3)]

    def ring3(k, p):
        axis, i = orders[p][2], pos(p, 2)
        return [rcopy(k, p, 8 + step, umid[k].at[p, (i + step) % RING], r3[k].at[p, step - 1], away(axis, step)) for step in (1, 2, 3)]

    def stage_a(k):
        pair_copy(k).wait_recv()
        r = ROW_CHUNKS[k]

        def block(e, carry):
            ye, xe = e // RING, e % RING
            for zz in range(RING):
                for p in range(3):
                    row = (zz * 3 + p) * r
                    mine = pl.ds(pl.multiple_of(core * (12 * r) + row, 8), r)
                    value = cbuf[k % 2, e, mine, :] + drecv[k][e, row : row + r, :]
                    at = {"x": xe, "y": ye, "z": zz}
                    sums[k][p, at[orders[p][0]], at[orders[p][1]], at[orders[p][2]]] = value
            return carry

        lax.fori_loop(0, eblocks, block, 0)
        for n in range(4):
            for p in range(3):
                ring1(k, p, (n,))[0].start()

    def stage_b(k):
        for p in range(3):
            i = pos(p, 0)
            up, down = (i + 1) % RING, (i + 3) % RING
            copies = ring1(k, p, (0, 1, 4, 5))
            copies[0].wait_recv()
            sums[k][p, up, 0:2] = sums[k][p, up, 0:2] + r1m[k][p, 0]
            copies[2].start()
            copies[1].wait_recv()
            sums[k][p, down, 2:4] = sums[k][p, down, 2:4] + r1m[k][p, 1]
            copies[3].start()

    def stage_c(k):
        for p in range(3):
            i = pos(p, 0)
            for copy in ring1(k, p, (2, 3, 4, 5)):
                copy.wait_recv()
            tmid[k][p] = sums[k][p, i] + r1f[k][p, 0] + r1f[k][p, 1]
            for copy in ring2(k, p):
                copy.start()

    def stage_d(k):
        for p in range(3):
            for copy in ring2(k, p):
                copy.wait_recv()
            umid[k][p] = tmid[k][p, pos(p, 1)] + r2[k][p, 0] + r2[k][p, 1] + r2[k][p, 2]
            for copy in ring3(k, p):
                copy.start()

    def stage_e(k):
        r = ROW_CHUNKS[k]
        for p in range(3):
            for copy in ring3(k, p):
                copy.wait_recv()
            row = 88 * p + offsets[k]
            fin[row : row + r, :] = umid[k][p, pos(p, 2)] + r3[k][p, 0] + r3[k][p, 1] + r3[k][p, 2]

    stages = (matmul_chunk, stage_a, stage_b, stage_c, stage_d, stage_e)
    for turn in range(chunks + len(stages) - 1):
        for lag, stage in enumerate(stages):
            if 0 <= turn - lag < chunks:
                stage(turn - lag)

    keep = keep_ref[pl.ds(ex, 1), :].astype(jnp.float32)
    rows = d_model // 8
    whole = fin[...] * keep
    first, second = whole[0:rows, :], whole[whole.shape[0] - rows :, :]
    out_ref[...] = jnp.transpose(jnp.where(core == 0, first, second))

    for stage in range(4):
        for copy in count_copies(stage):
            copy.wait_send()
    for k in range(max(chunks - 2, 0), chunks):
        pair_copy(k).wait_send()
    for k in range(chunks):
        for p in range(3):
            for copy in ring1(k, p, range(6)) + ring2(k, p) + ring3(k, p):
                copy.wait_send()


def solution(mesh):
    devices = mesh.devices.size

    def local(tokens, router_logits, gate_grad, expert_index, keep_mask):
        tok_rows, d_model = tokens.shape
        experts = router_logits.shape[1]
        eblocks = experts // LANES
        chunks = len(ROW_CHUNKS)
        f32, bf16, i32 = jnp.float32, jnp.bfloat16, jnp.int32
        rmax = max(ROW_CHUNKS)
        vm = pltpu.VMEM

        def per_chunk(shape_of):
            return [vm(shape_of(r), f32) for r in ROW_CHUNKS]

        scratch = [
            vm((2, TB, experts), bf16),
            vm((2, TB, d_model), bf16),
            vm((tok_rows, LANES), i32),
            vm((tok_rows, LANES), f32),
            vm((tok_rows, LANES), f32),
            vm((tok_rows, experts), f32),
            vm((2, tok_rows, experts), bf16),
            vm((d_model, TB), f32),
            vm((24 * sum(ROW_CHUNKS), tok_rows), bf16),
            vm((2, eblocks, 24 * rmax, LANES), f32),
            per_chunk(lambda r: (eblocks, 12 * r, LANES)),
            per_chunk(lambda r: (3, 4, 4, 4, r, LANES)),
            per_chunk(lambda r: (3, 2, 2, 4, r, LANES)),
            per_chunk(lambda r: (3, 2, 4, 4, r, LANES)),
            per_chunk(lambda r: (3, 4, 4, r, LANES)),
            per_chunk(lambda r: (3, 3, 4, r, LANES)),
            per_chunk(lambda r: (3, 4, r, LANES)),
            per_chunk(lambda r: (3, 3, r, LANES)),
            vm((264, LANES), f32),
            vm((4, eblocks, LANES), i32),
            vm((10, eblocks, LANES), i32),
            vm((eblocks, LANES), f32),
            pltpu.SemaphoreType.DMA((2,)),
            pltpu.SemaphoreType.DMA((2,)),
            pltpu.SemaphoreType.DMA((10,)),
            pltpu.SemaphoreType.DMA((10,)),
            pltpu.SemaphoreType.DMA((chunks,)),
            pltpu.SemaphoreType.DMA((chunks,)),
            pltpu.SemaphoreType.DMA((chunks, 3, 12)),
            pltpu.SemaphoreType.DMA((chunks, 3, 12)),
        ]
        return pl.pallas_call(
            functools.partial(kernel, tok_rows * devices),
            out_shape=jax.ShapeDtypeStruct((LANES, d_model // 8), f32),
            in_specs=[pl.BlockSpec(memory_space=pltpu.VMEM)] * 3 + [pl.BlockSpec(memory_space=pl.ANY)] * 2,
            out_specs=pl.BlockSpec(memory_space=pltpu.VMEM),
            scratch_shapes=scratch,
            compiler_params=pltpu.CompilerParams(collective_id=0, has_side_effects=True, vmem_limit_bytes=67043328),
        )(
            expert_index.reshape(tok_rows // LANES, LANES),
            gate_grad.reshape(tok_rows // LANES, LANES),
            keep_mask.reshape(eblocks, LANES),
            tokens,
            router_logits,
        )

    return jax.shard_map(
        local,
        mesh=mesh,
        in_specs=(P(("dp", "expert"), None), P(("dp", "expert"), None), P(("dp", "expert")), P(("dp", "expert"), None), P()),
        out_specs=P("expert", "dp"),
        check_vma=False,
    )
```

time: 245 us -> 92.3 us (0.38)
  waiting for transfers between devices: 108 us -> 0 us
  Pallas kernels: 0 us -> 83.9 us
  blocking collectives: 50.6 us -> 0 us
  matrix products: 41.4 us -> 0 us
  other arithmetic: 21.9 us -> 0 us
  between operations: 13.4 us -> 0.01 us
    reduce_scatter x1 -> x0, waiting for transfers between devices: 108 us -> none  [local(): lax.psum_scatter(make_term(logit_grad, wide_tokens), EXPERT, scatter_dime...]
    pallas_call x0 -> x1, Pallas kernels: none -> 83.9 us  [local(): pl.pallas_call(functools.partial(kernel, tok_rows * devices), out_shape=j...]
    dot_general x3 -> x0, matrix products: 41.4 us -> none  [the longest x1 32.6 us: make_term(): lax.dot_general(grad_source, wide_tokens, (((0,), (0,)), ((), ())), preci...]
    psum x4 -> x0, blocking collectives: 30 us -> none  [over_axes(): value = lax.psum(value, axis)]
    all_to_all x1 -> x0, blocking collectives: 20.6 us -> none  [sent_and_summed(): lax.all_to_all(in_blocks(value, dim, devices), axis, 0, 0, tiled=True)]
    reduce_sum x8 -> x0, other arithmetic: 10.4 us -> none  [the longest x2 5.13 us: block_grad(): router_probs = weights / jnp.sum(weights, axis=1, keepdims=True)]
    while x16 -> x0, local copies, waits for them, and re-layouts: 6.45 us -> none
    unnamed x1, local copies, waits for them, and re-layouts: 0.5 us -> 6.44 us
  transfers between devices with their start and end apart: 1 -> 0, of which waited for: 1 -> 0; matrix products, arithmetic and copies ran while one was open for 0% -> 0% of each run, Pallas kernels for 0% -> 0%
where the time goes in v1:
time: 92.3 us; the launch traced here: 92 us
  Pallas kernels  83.9 us (91%)
  local copies, waits for them, and re-layouts  8.12 us (9%)
    pallas_call x1, Pallas kernels, local(): pl.pallas_call(functools.partial(kernel, tok_rows * devices), out_shape=j...  83.9 us
    unnamed x1, local copies, waits for them, and re-layouts  6.44 us

profile of v1, /device:TPU:0, one launch (start us, length us, event | category | flops | bytes accessed | tf_op | source)
XLA Modules:
  0.0 92.0 jit_solution(340045837213837288)
XLA Ops:
  0.0 6.4 %copy.6.tok_ref = bf16[1024,2080]{1,0:T(8,128)(2,1)} copy(bf16[1024,2080]{0,1:T(8,128)(2,1)} %param.5) | data formatting | bytes 8519680 | tf_op args[0]
  6.4 83.9 %shard_map.55 = f32[128,260]{1,0:T(8,128)} custom-call(s32[8,128]{1,0:T(8,128)} %bitcast.4, f32[8,128]{1,0:T(8,128)} %bitcast.5, s32[16,128]{1,0:T(8,128)} %bitcast.3, bf16[1024,2080]{1,0:T(8,128)(2,1)} %copy.6.tok_ref, bf16[1024,2048]{1,0:T(8,128)(2,1)} %logit_ref.1), custom_call_target="tpu_custom_call" | custom-call | tf_op jit(solution)/shard_map/pallas_call | solution.py:387
  90.3 1.7 %copy.7 = f32[128,260]{0,1:T(8,128)} copy(f32[128,260]{1,0:T(8,128)} %shard_map.55) | data formatting | bytes 266240 | tf_op jit(solution)/shard_map/pallas_call | solution.py:387

commit v2 on v1

--- a/solution.py
+++ b/solution.py
@@ -15,10 +15,10 @@
 
 
 def kernel(total_tokens, idx_ref, gate_ref, keep_ref, tok_ref, logit_ref, out_ref,
-           lbuf, xbuf, icol, acol, invc, ptab, gmat, xf, xt, cbuf, drecv, sums, r1m, r1f, tmid, r2, umid, r3,
+           lbuf, icol, acol, invc, ptab, gmat, xt, cbuf, drecv, sums, r1m, r1f, tmid, r2, umid, r3,
            fin, cnt, cnt_recv, aux_ref,
            lsem, xsem, csend, crecv, dsend, drsem, ssem, rsem):
-    tok_rows, d_model = tok_ref.shape
+    d_model, tok_rows = tok_ref.shape
     experts = logit_ref.shape[1]
     eblocks = experts // LANES
     blocks = tok_rows // TB
@@ -43,13 +43,16 @@
     def load_logits(b, slot):
         return pltpu.make_async_copy(logit_ref.at[pl.ds(b * TB, TB), :], lbuf.at[slot], lsem.at[slot])
 
-    def load_tokens(b, slot):
-        return pltpu.make_async_copy(tok_ref.at[pl.ds(b * TB, TB), :], xbuf.at[slot], xsem.at[slot])
+    for k in range(chunks):
+        r = ROW_CHUNKS[k]
+        for group in range(24):
+            cc, zz, part = group // 12, (group // 3) % 4, group % 3
+            src = (d_model // RING) * zz + 256 * cc + 88 * part + offsets[k]
+            dst = 24 * offsets[k] + r * group
+            pltpu.make_async_copy(tok_ref.at[pl.ds(src, r), :], xt.at[pl.ds(dst, r), :], xsem.at[k]).start()
 
     load_logits(0, 0).start()
     load_logits(1, 1).start()
-    load_tokens(0, 0).start()
-    load_tokens(1, 1).start()
 
     barrier = pltpu.get_barrier_semaphore()
     peers = [sibling] + [away(axis, step) for axis in "xyz" for step in (1, 2, 3)]
@@ -132,40 +135,12 @@
 
         lax.fori_loop(0, TB // RS, rows, 0)
 
-    def xpose_block(b):
-        slot = b % 2
-        load_tokens(b, slot).wait()
-        for c in range(0, d_model, LANES):
-            width = min(LANES, d_model - c)
-            xf[c : c + width, :] = jnp.transpose(xbuf[slot, :, c : c + width].astype(jnp.float32))
-        cols = pl.ds(pl.multiple_of(b * TB, TB), TB)
-        for k in range(chunks):
-            r = ROW_CHUNKS[k]
-            pieces = []
-            for group in range(24):
-                cc, zz, part = group // 12, (group // 3) % 4, group % 3
-                src = (d_model // RING) * zz + 256 * cc + 88 * part + offsets[k]
-                pieces.append(xf[src : src + r, :])
-            dst = 24 * offsets[k]
-            if r == 8:
-                for g in range(0, 24, 2):
-                    xt[dst + 8 * g : dst + 8 * g + 16, cols] = jnp.concatenate([pieces[g], pieces[g + 1]], axis=0).astype(jnp.bfloat16)
-            else:
-                for g in range(24):
-                    xt[dst + r * g : dst + r * (g + 1), cols] = pieces[g].astype(jnp.bfloat16)
-
     def prep(b, carry):
         stats_block(b)
 
         @pl.when(b + 2 < blocks)
         def _():
             load_logits(b + 2, b % 2).start()
-
-        xpose_block(b)
-
-        @pl.when(b + 2 < blocks)
-        def _():
-            load_tokens(b + 2, b % 2).start()
 
         return carry
 
@@ -212,6 +187,8 @@
             pair_copy(k - 2).wait_send()
         rows = 24 * ROW_CHUNKS[k]
         base = 24 * offsets[k]
+        chunk_rows = xt.at[pl.ds(base, rows), :]
+        pltpu.make_async_copy(chunk_rows, chunk_rows, xsem.at[k]).wait()
 
         def tile(n, carry):
             cols = pl.ds(pl.multiple_of(n * NT, NT), NT)
@@ -324,7 +301,7 @@
     rows = d_model // 8
     whole = fin[...] * keep
     first, second = whole[0:rows, :], whole[whole.shape[0] - rows :, :]
-    out_ref[...] = jnp.transpose(jnp.where(core == 0, first, second))
+    out_ref[...] = jnp.where(core == 0, first, second)
 
     for stage in range(4):
         for copy in count_copies(stage):
@@ -354,13 +331,11 @@
 
         scratch = [
             vm((2, TB, experts), bf16),
-            vm((2, TB, d_model), bf16),
             vm((tok_rows, LANES), i32),
             vm((tok_rows, LANES), f32),
             vm((tok_rows, LANES), f32),
             vm((tok_rows, experts), f32),
             vm((2, tok_rows, experts), bf16),
-            vm((d_model, TB), f32),
             vm((24 * sum(ROW_CHUNKS), tok_rows), bf16),
             vm((2, eblocks, 24 * rmax, LANES), f32),
             per_chunk(lambda r: (eblocks, 12 * r, LANES)),
@@ -376,7 +351,7 @@
             vm((10, eblocks, LANES), i32),
             vm((eblocks, LANES), f32),
             pltpu.SemaphoreType.DMA((2,)),
-            pltpu.SemaphoreType.DMA((2,)),
+            pltpu.SemaphoreType.DMA((chunks,)),
             pltpu.SemaphoreType.DMA((10,)),
             pltpu.SemaphoreType.DMA((10,)),
             pltpu.SemaphoreType.DMA((chunks,)),
@@ -386,7 +361,7 @@
         ]
         return pl.pallas_call(
             functools.partial(kernel, tok_rows * devices),
-            out_shape=jax.ShapeDtypeStruct((LANES, d_model // 8), f32),
+            out_shape=jax.ShapeDtypeStruct((d_model // 8, LANES), f32),
             in_specs=[pl.BlockSpec(memory_space=pltpu.VMEM)] * 3 + [pl.BlockSpec(memory_space=pl.ANY)] * 2,
             out_specs=pl.BlockSpec(memory_space=pltpu.VMEM),
             scratch_shapes=scratch,
@@ -395,9 +370,9 @@
             expert_index.reshape(tok_rows // LANES, LANES),
             gate_grad.reshape(tok_rows // LANES, LANES),
             keep_mask.reshape(eblocks, LANES),
-            tokens,
+            tokens.T,
             router_logits,
-        )
+        ).T
 
     return jax.shard_map(
         local,

time: 92.3 us -> 85.6 us (0.927)
  local copies, waits for them, and re-layouts: 8.12 us -> 1.57 us
    unnamed x1, local copies, waits for them, and re-layouts: 6.44 us -> 1.57 us
    pallas_call x1 -> x0, local copies, waits for them, and re-layouts: 1.69 us -> none  [local(): pl.pallas_call(functools.partial(kernel, tok_rows * devices), out_shape=j...]
where the time goes in v2:
time: 85.6 us; the launch traced here: 85.3 us
  Pallas kernels  83.8 us (98%)
  local copies, waits for them, and re-layouts  1.57 us (2%)
    pallas_call x1, Pallas kernels, local(): pl.pallas_call(functools.partial(kernel, tok_rows * devices), out_shape=j...  83.8 us

profile of v2, /device:TPU:0, one launch (start us, length us, event | category | flops | bytes accessed | tf_op | source)
XLA Modules:
  0.0 85.3 jit_solution(2724249370565061572)
XLA Ops:
  0.0 83.8 %shard_map.55 = f32[260,128]{1,0:T(8,128)} custom-call(s32[8,128]{1,0:T(8,128)} %bitcast.8, f32[8,128]{1,0:T(8,128)} %bitcast.9, s32[16,128]{1,0:T(8,128)} %bitcast.7, bf16[2080,1024]{1,0:T(8,128)(2,1)} %bitcast.5, bf16[1024,2048]{1,0:T(8,128)(2,1)} %logit_ref.1), custom_call_target="tpu_custom_call" | custom-call | tf_op jit(solution)/shard_map/pallas_call | solution.py:362
  83.8 1.6 %copy.7 = f32[128,260]{0,1:T(8,128)} copy(f32[128,260]{0,1:T(8,128)} %bitcast.6) | data formatting | bytes 266240

commit v3 on v2

v3 whole, which is shorter than its diff:
```python
import functools

import jax
import jax.numpy as jnp
from jax import lax
from jax.experimental import pallas as pl
from jax.experimental.pallas import tpu as pltpu
from jax.sharding import PartitionSpec as P

MESH = pl.DeviceIdType.MESH
RING = 4
LANES = 128
ROW_CHUNKS = (8, 16, 16, 16, 16, 16)
TB = 128


def kernel(total_tokens, idx_ref, gate_ref, keep_ref, tok_ref, logit_ref, out_ref,
           lbuf, icol, acol, drop, ptab, gmat, xt, cbuf, drecv, sums, r1m, r1f, tmid, r2m, r2f, umid, r3,
           fin, cnt, cnt_recv, aux_ref,
           lsem, xsem, csend, crecv, dsend, drsem, ssem, rsem):
    d_model, tok_rows = tok_ref.shape
    experts = logit_ref.shape[1]
    eblocks = experts // LANES
    blocks = tok_rows // TB
    chunks = len(ROW_CHUNKS)
    offsets = [sum(ROW_CHUNKS[:k]) for k in range(chunks)]

    dp = lax.axis_index("dp")
    ex = lax.axis_index("expert")
    zc, core = dp // 2, dp % 2
    yc, xc = ex // RING, ex % RING
    here = {"x": xc, "y": yc, "z": zc}

    def device(**moved):
        at = dict(here, **moved)
        return (2 * at["z"] + core, RING * at["y"] + at["x"])

    sibling = (2 * zc + 1 - core, ex)
    same_column = [((dp + step) % 8, ex) for step in range(1, 8)]

    def away(axis, step):
        return device(**{axis: (here[axis] + step) % RING})

    def load_logits(b, slot):
        return pltpu.make_async_copy(logit_ref.at[pl.ds(b * TB, TB), :], lbuf.at[slot], lsem.at[slot])

    for k in range(chunks):
        r = ROW_CHUNKS[k]
        for group in range(24):
            cc, zz, part = group // 12, (group // 3) % 4, group % 3
            src = (d_model // RING) * zz + 256 * cc + 88 * part + offsets[k]
            dst = 24 * offsets[k] + r * group
            pltpu.make_async_copy(tok_ref.at[pl.ds(src, r), :], xt.at[pl.ds(dst, r), :], xsem.at[k]).start()

    load_logits(0, 0).start()
    load_logits(1, 1).start()

    barrier = pltpu.get_barrier_semaphore()
    peers = same_column + [away(axis, step) for axis in "xy" for step in (1, 2, 3)]
    for peer in peers:
        pl.semaphore_signal(barrier, inc=1, device_id=peer, device_id_type=MESH)

    idx = idx_ref[...]
    total = jnp.zeros((eblocks, LANES), jnp.float32)
    for b in range(blocks):
        row = idx[b : b + 1, :]
        high = (row // LANES == lax.broadcasted_iota(jnp.int32, (eblocks, LANES), 0)).astype(jnp.bfloat16)
        low = (row % LANES == lax.broadcasted_iota(jnp.int32, (LANES, LANES), 0)).astype(jnp.bfloat16)
        total = total + lax.dot_general(high, low, (((1,), (1,)), ((), ())), preferred_element_type=jnp.float32)
    cnt[0] = total.astype(jnp.int32)

    def count_copies(stage):
        targets = same_column if stage == 0 else [away("xy"[stage - 1], step) for step in (1, 2, 3)]
        first = (0, 7, 10)[stage]
        return [
            pltpu.make_async_remote_copy(cnt.at[stage], cnt_recv.at[first + n], csend.at[stage], crecv.at[first + n], device_id=target, device_id_type=MESH)
            for n, target in enumerate(targets)
        ]

    def count_arrive(stage):
        value = cnt[stage]
        for number, copy in enumerate(count_copies(stage)):
            copy.wait_recv()
            value = value + cnt_recv[(0, 7, 10)[stage] + number]
        return value

    def count_step(stage):
        cnt[stage + 1] = count_arrive(stage)
        for copy in count_copies(stage + 1):
            copy.start()

    idx_t = jnp.transpose(idx.astype(jnp.float32))
    gate_t = jnp.transpose(gate_ref[...])
    for b in range(blocks):
        icol[b * TB : (b + 1) * TB, :] = jnp.broadcast_to(idx_t[:, b : b + 1], (TB, LANES)).astype(jnp.int32)
        acol[b * TB : (b + 1) * TB, :] = jnp.broadcast_to(gate_t[:, b : b + 1], (TB, LANES))

    RS = 32

    def lane_of(j):
        return lax.broadcasted_iota(jnp.int32, (RS, LANES), 1) + j * LANES

    def stats_block(b):
        slot = b % 2
        load_logits(b, slot).wait()

        def rows(r, carry):
            local = pl.ds(pl.multiple_of(r * RS, RS), RS)
            at = pl.ds(pl.multiple_of(b * TB + r * RS, RS), RS)
            peak = lbuf[slot, local, 0:LANES].astype(jnp.float32)
            for j in range(1, eblocks):
                peak = jnp.maximum(peak, lbuf[slot, local, j * LANES : (j + 1) * LANES].astype(jnp.float32))
            peak = jnp.max(peak, axis=1, keepdims=True)
            mass = jnp.zeros((RS, LANES), jnp.float32)
            top = jnp.zeros((RS, LANES), jnp.float32)
            chosen = icol[at, :]
            for j in range(eblocks):
                weight = jnp.exp(lbuf[slot, local, j * LANES : (j + 1) * LANES].astype(jnp.float32) - peak)
                ptab[at, j * LANES : (j + 1) * LANES] = weight
                mass = mass + weight
                top = top + jnp.where(chosen == lane_of(j), weight, 0.0)
            inverse = 1.0 / jnp.sum(mass, axis=1, keepdims=True)
            top_prob = jnp.sum(top, axis=1, keepdims=True) * inverse
            acol[at, :] = acol[at, :] * top_prob
            for j in range(eblocks):
                ptab[at, j * LANES : (j + 1) * LANES] = ptab[at, j * LANES : (j + 1) * LANES] * inverse
            return carry

        lax.fori_loop(0, TB // RS, rows, 0)

    def prep(b, carry):
        stats_block(b)

        @pl.when(b + 2 < blocks)
        def _():
            load_logits(b + 2, b % 2).start()

        return carry

    with jax.named_scope("prep_0"):
        lax.fori_loop(0, 3, prep, 0)
    with jax.named_scope("barrier"):
        pl.semaphore_wait(barrier, len(peers))
    for copy in count_copies(0):
        copy.start()
    with jax.named_scope("prep_1"):
        lax.fori_loop(3, 6, prep, 0)
    with jax.named_scope("count_step_0"):
        count_step(0)
    with jax.named_scope("prep_2"):
        lax.fori_loop(6, 8, prep, 0)
    with jax.named_scope("count_step_1"):
        count_step(1)
    with jax.named_scope("count_last"):
        aux_ref[...] = count_arrive(2).astype(jnp.float32) * (experts / total_tokens)

    def spread_rows(r, carry):
        at = pl.ds(pl.multiple_of(r * RS, RS), RS)
        acc = ptab[at, 0:LANES] * aux_ref[0:1, :]
        for j in range(1, eblocks):
            acc = acc + ptab[at, j * LANES : (j + 1) * LANES] * aux_ref[j : j + 1, :]
        drop[at, :] = jnp.sum(acc, axis=1, keepdims=True) + acol[at, :]
        return carry

    with jax.named_scope("spread"):
        lax.fori_loop(0, tok_rows // RS, spread_rows, 0, unroll=4)

    def grad_quarter(q):
        for row in range(0, tok_rows, RS):
            gain = acol[row : row + RS, :]
            less = drop[row : row + RS, :]
            chosen = icol[row : row + RS, :]
            for j in range(RING * q, RING * q + RING):
                value = ptab[row : row + RS, j * LANES : (j + 1) * LANES] * (aux_ref[j : j + 1, :] - less)
                value = jnp.where(chosen == lane_of(j), value + gain, value)
                big = value.astype(jnp.bfloat16)
                cols = slice((j - RING * q) * LANES, (j - RING * q + 1) * LANES)
                gmat[q][0, row : row + RS, cols] = big
                gmat[q][1, row : row + RS, cols] = (value - big.astype(jnp.float32)).astype(jnp.bfloat16)

    def pair_copy(k, first, count):
        rows = 12 * ROW_CHUNKS[k]
        src = cbuf.at[k % 2, pl.ds(first, count), pl.ds(pl.multiple_of((1 - core) * rows, 8), rows), :]
        return pltpu.make_async_remote_copy(
            src, drecv[k].at[pl.ds(first, count)], dsend.at[k], drsem.at[k], device_id=sibling, device_id_type=MESH)

    def matmul_quarter(k, q):
        rows = 24 * ROW_CHUNKS[k]
        base = 24 * offsets[k]
        if q == 0:
            if k >= 2:
                pair_copy(k - 2, 0, eblocks).wait_send()
            chunk_rows = xt.at[pl.ds(base, rows), :]
            pltpu.make_async_copy(chunk_rows, chunk_rows, xsem.at[k]).wait()
        left = xt[base : base + rows, :]
        value = jnp.dot(left, gmat[q][0], preferred_element_type=jnp.float32)
        value = value + jnp.dot(left, gmat[q][1], preferred_element_type=jnp.float32)
        for j in range(RING):
            cbuf[k % 2, RING * q + j, 0:rows, :] = value[:, j * LANES : (j + 1) * LANES]
        pair_copy(k, RING * q, RING).start()

    orders = ("xyz", "yzx", "zxy")

    def pos(p, stage):
        return here[orders[p][stage]]

    def around(k, p, stage, numbers):
        axis, i = orders[p][stage], pos(p, stage)
        up, down, far = (i + 1) % RING, (i + 3) % RING, (i + 2) % RING
        right, left = away(axis, 1), away(axis, 3)
        s = (sums, tmid)[stage][k].at[p]
        m = (r1m, r2m)[stage][k].at[p]
        f = (r1f, r2f)[stage][k].at[p]
        table = (
            (s.at[far, 0:2], m.at[0], 0, right),
            (s.at[far, 2:4], m.at[1], 1, left),
            (s.at[up, 2:4], f.at[0, 2:4], 2, right),
            (s.at[down, 0:2], f.at[1, 0:2], 2, left),
            (s.at[up, 0:2], f.at[0, 0:2], 2, right),
            (s.at[down, 2:4], f.at[1, 2:4], 2, left),
        )
        copies = []
        for n in numbers:
            src, dst, sem, peer = table[n]
            copies.append(pltpu.make_async_remote_copy(src, dst, ssem.at[k, stage], rsem.at[k, p, 3 * stage + sem], device_id=peer, device_id_type=MESH))
        return copies

    def last_ring(k, p):
        axis, i = orders[p][2], pos(p, 2)
        return [
            pltpu.make_async_remote_copy(
                umid[k].at[p, (i + step) % RING], r3[k].at[p, step - 1], ssem.at[k, 2], rsem.at[k, p, 6], device_id=away(axis, step), device_id_type=MESH)
            for step in (1, 2, 3)
        ]

    def taken(ref, sem):
        pltpu.make_async_copy(ref, ref, sem).wait()

    def merge(k, p, stage):
        i = pos(p, stage)
        up, down = (i + 1) % RING, (i + 3) % RING
        s, m = (sums, tmid)[stage][k], (r1m, r2m)[stage][k]
        first, second, third, fourth = around(k, p, stage, (0, 1, 4, 5))
        first.wait_recv()
        s[p, up, 0:2] = s[p, up, 0:2] + m[p, 0]
        third.start()
        second.wait_recv()
        s[p, down, 2:4] = s[p, down, 2:4] + m[p, 1]
        fourth.start()

    def stage_a(k):
        pair_copy(k, 0, eblocks).wait_recv()
        r = ROW_CHUNKS[k]

        def block(e, carry):
            ye, xe = e // RING, e % RING
            for zz in range(RING):
                for p in range(3):
                    row = (zz * 3 + p) * r
                    mine = pl.ds(pl.multiple_of(core * (12 * r) + row, 8), r)
                    value = cbuf[k % 2, e, mine, :] + drecv[k][e, row : row + r, :]
                    at = {"x": xe, "y": ye, "z": zz}
                    sums[k][p, at[orders[p][0]], at[orders[p][1]], at[orders[p][2]]] = value
            return carry

        lax.fori_loop(0, eblocks, block, 0)
        for n in range(4):
            for p in range(3):
                around(k, p, 0, (n,))[0].start()

    def stage_b(k):
        for p in range(3):
            merge(k, p, 0)

    def stage_c(k):
        for p in range(3):
            taken(r1f[k].at[p], rsem.at[k, p, 2])
            tmid[k][p] = sums[k][p, pos(p, 0)] + r1f[k][p, 0] + r1f[k][p, 1]
            for copy in around(k, p, 1, (0, 1, 2, 3)):
                copy.start()

    def stage_d(k):
        for p in range(3):
            merge(k, p, 1)

    def stage_e(k):
        for p in range(3):
            taken(r2f[k].at[p], rsem.at[k, p, 5])
            umid[k][p] = tmid[k][p, pos(p, 1)] + r2f[k][p, 0] + r2f[k][p, 1]
            for copy in last_ring(k, p):
                copy.start()
        taken(sums[k].at[:, 0:3], ssem.at[k, 0])

    def stage_f(k):
        r = ROW_CHUNKS[k]
        for p in range(3):
            taken(r3[k].at[p], rsem.at[k, p, 6])
            row = 88 * p + offsets[k]
            fin[row : row + r, :] = umid[k][p, pos(p, 2)] + r3[k][p, 0] + r3[k][p, 1] + r3[k][p, 2]
        taken(tmid[k].at[:, 0:3], ssem.at[k, 1])

    plan = []
    for k in range(chunks):
        for q in range(RING):
            plan.append((RING * k + q, -1, k, "matmul", functools.partial(matmul_quarter, k, q)))
        for order, (stage, lag) in enumerate(((stage_a, 2), (stage_b, 5), (stage_c, 9), (stage_d, 12), (stage_e, 15), (stage_f, 18))):
            plan.append((RING * k + 3 + lag, order, k, stage.__name__, functools.partial(stage, k)))
    with jax.named_scope("first_chunk"):
        for q in range(RING):
            grad_quarter(q)
            if q:
                matmul_quarter(0, q - 1)
        matmul_quarter(0, RING - 1)
    for when, order, k, name, step in sorted(plan, key=lambda entry: entry[:3]):
        if when >= RING:
            with jax.named_scope(f"{name}_{k}"):
                step()

    keep = keep_ref[pl.ds(ex, 1), :].astype(jnp.float32)
    rows = d_model // 8
    whole = fin[...] * keep
    first, second = whole[0:rows, :], whole[whole.shape[0] - rows :, :]
    out_ref[...] = jnp.where(core == 0, first, second)

    taken(cnt_recv.at[0:7], csend.at[0])
    taken(cnt_recv.at[0:3], csend.at[1])
    taken(cnt_recv.at[0:3], csend.at[2])
    for k in range(max(chunks - 2, 0), chunks):
        pair_copy(k, 0, eblocks).wait_send()
    for k in range(chunks):
        taken(umid[k].at[:, 0:3], ssem.at[k, 2])


def solution(mesh):
    devices = mesh.devices.size

    def local(tokens, router_logits, gate_grad, expert_index, keep_mask):
        tok_rows, d_model = tokens.shape
        experts = router_logits.shape[1]
        eblocks = experts // LANES
        chunks = len(ROW_CHUNKS)
        f32, bf16, i32 = jnp.float32, jnp.bfloat16, jnp.int32
        rmax = max(ROW_CHUNKS)
        vm = pltpu.VMEM

        def per_chunk(shape_of):
            return [vm(shape_of(r), f32) for r in ROW_CHUNKS]

        scratch = [
            vm((2, TB, experts), bf16),
            vm((tok_rows, LANES), i32),
            vm((tok_rows, LANES), f32),
            vm((tok_rows, LANES), f32),
            vm((tok_rows, experts), f32),
            [vm((2, tok_rows, experts // RING), bf16)] * RING,
            vm((24 * sum(ROW_CHUNKS), tok_rows), bf16),
            vm((2, eblocks, 24 * rmax, LANES), f32),
            per_chunk(lambda r: (eblocks, 12 * r, LANES)),
            per_chunk(lambda r: (3, 4, 4, 4, r, LANES)),
            per_chunk(lambda r: (3, 2, 2, 4, r, LANES)),
            per_chunk(lambda r: (3, 2, 4, 4, r, LANES)),
            per_chunk(lambda r: (3, 4, 4, r, LANES)),
            per_chunk(lambda r: (3, 2, 2, r, LANES)),
            per_chunk(lambda r: (3, 2, 4, r, LANES)),
            per_chunk(lambda r: (3, 4, r, LANES)),
            per_chunk(lambda r: (3, 3, r, LANES)),
            vm((264, LANES), f32),
            vm((3, eblocks, LANES), i32),
            vm((13, eblocks, LANES), i32),
            vm((eblocks, LANES), f32),
            pltpu.SemaphoreType.DMA((2,)),
            pltpu.SemaphoreType.DMA((chunks,)),
            pltpu.SemaphoreType.DMA((3,)),
            pltpu.SemaphoreType.DMA((13,)),
            pltpu.SemaphoreType.DMA((chunks,)),
            pltpu.SemaphoreType.DMA((chunks,)),
            pltpu.SemaphoreType.DMA((chunks, 3)),
            pltpu.SemaphoreType.DMA((chunks, 3, 7)),
        ]
        return pl.pallas_call(
            functools.partial(kernel, tok_rows * devices),
            out_shape=jax.ShapeDtypeStruct((d_model // 8, LANES), f32),
            in_specs=[pl.BlockSpec(memory_space=pltpu.VMEM)] * 3 + [pl.BlockSpec(memory_space=pl.ANY)] * 2,
            out_specs=pl.BlockSpec(memory_space=pltpu.VMEM),
            scratch_shapes=scratch,
            compiler_params=pltpu.CompilerParams(collective_id=0, has_side_effects=True, vmem_limit_bytes=67043328),
        )(
            expert_index.reshape(tok_rows // LANES, LANES),
            gate_grad.reshape(tok_rows // LANES, LANES),
            keep_mask.reshape(eblocks, LANES),
            tokens.T,
            router_logits,
        ).T

    return jax.shard_map(
        local,
        mesh=mesh,
        in_specs=(P(("dp", "expert"), None), P(("dp", "expert"), None), P(("dp", "expert")), P(("dp", "expert"), None), P()),
        out_specs=P("expert", "dp"),
        check_vma=False,
    )
```

time: 85.6 us -> 84 us (0.981)
  Pallas kernels: 83.8 us -> 82.1 us
    pallas_call x1, Pallas kernels: 83.8 us -> 82.1 us  [local(): pl.pallas_call(functools.partial(kernel, tok_rows * devices), out_shape=j...]
where the time goes in v3:
time: 84 us; the launch traced here: 83.7 us
  Pallas kernels  82.1 us (98%)
  local copies, waits for them, and re-layouts  1.57 us (2%)
    pallas_call x1, Pallas kernels, local(): pl.pallas_call(functools.partial(kernel, tok_rows * devices), out_shape=j...  82.1 us

profile of v3, /device:TPU:0, one launch (start us, length us, event | category | flops | bytes accessed | tf_op | source)
XLA Modules:
  0.0 83.7 jit_solution(3564676343157746426)
XLA Ops:
  0.0 82.1 %shard_map.55 = f32[260,128]{1,0:T(8,128)} custom-call(s32[8,128]{1,0:T(8,128)} %bitcast.8, f32[8,128]{1,0:T(8,128)} %bitcast.9, s32[16,128]{1,0:T(8,128)} %bitcast.7, bf16[2080,1024]{1,0:T(8,128)(2,1)} %bitcast.5, bf16[1024,2048]{1,0:T(8,128)(2,1)} %logit_ref.1), custom_call_target="tpu_custom_call" | custom-call | tf_op jit(solution)/shard_map/pallas_call | solution.py:380
  82.1 1.6 %copy.7 = f32[128,260]{0,1:T(8,128)} copy(f32[128,260]{0,1:T(8,128)} %bitcast.6) | data formatting | bytes 266240

commit v4 on v3

--- a/solution.py
+++ b/solution.py
@@ -9,13 +9,17 @@
 
 MESH = pl.DeviceIdType.MESH
 RING = 4
+PAIR_TIME, HOP_TIME, QUARTER_TIME = 1.5, 2.4, 0.0606
+PLANE = (5, 6)
+EARLY_OWN = 6
 LANES = 128
-ROW_CHUNKS = (8, 16, 16, 16, 16, 16)
+ROW_CHUNKS = (8, 8, 16, 16, 16, 16, 8)
 TB = 128
+SLOTS = 3
 
 
 def kernel(total_tokens, idx_ref, gate_ref, keep_ref, tok_ref, logit_ref, out_ref,
-           lbuf, icol, acol, drop, ptab, gmat, xt, cbuf, drecv, sums, r1m, r1f, tmid, r2m, r2f, umid, r3,
+           lbuf, icol, acol, drop, ptab, gmat, xt, cbuf, drecv, sums, r1m, r1f, tmid, r2m, r2f, umid, r3, plane,
            fin, cnt, cnt_recv, aux_ref,
            lsem, xsem, csend, crecv, dsend, drsem, ssem, rsem):
     d_model, tok_rows = tok_ref.shape
@@ -44,16 +48,8 @@
     def load_logits(b, slot):
         return pltpu.make_async_copy(logit_ref.at[pl.ds(b * TB, TB), :], lbuf.at[slot], lsem.at[slot])
 
-    for k in range(chunks):
-        r = ROW_CHUNKS[k]
-        for group in range(24):
-            cc, zz, part = group // 12, (group // 3) % 4, group % 3
-            src = (d_model // RING) * zz + 256 * cc + 88 * part + offsets[k]
-            dst = 24 * offsets[k] + r * group
-            pltpu.make_async_copy(tok_ref.at[pl.ds(src, r), :], xt.at[pl.ds(dst, r), :], xsem.at[k]).start()
-
-    load_logits(0, 0).start()
-    load_logits(1, 1).start()
+    for b in range(SLOTS):
+        load_logits(b, b).start()
 
     barrier = pltpu.get_barrier_semaphore()
     peers = same_column + [away(axis, step) for axis in "xy" for step in (1, 2, 3)]
@@ -101,7 +97,7 @@
         return lax.broadcasted_iota(jnp.int32, (RS, LANES), 1) + j * LANES
 
     def stats_block(b):
-        slot = b % 2
+        slot = b % SLOTS
         load_logits(b, slot).wait()
 
         def rows(r, carry):
@@ -131,24 +127,33 @@
     def prep(b, carry):
         stats_block(b)
 
-        @pl.when(b + 2 < blocks)
+        @pl.when(b + SLOTS < blocks)
         def _():
-            load_logits(b + 2, b % 2).start()
+            load_logits(b + SLOTS, b % SLOTS).start()
 
         return carry
 
     with jax.named_scope("prep_0"):
-        lax.fori_loop(0, 3, prep, 0)
+        lax.fori_loop(0, 2, prep, 0)
     with jax.named_scope("barrier"):
         pl.semaphore_wait(barrier, len(peers))
     for copy in count_copies(0):
         copy.start()
+
+    for k in range(chunks):
+        r = ROW_CHUNKS[k]
+        for group in range(24):
+            cc, zz, part = group // 12, (group // 3) % 4, group % 3
+            src = (d_model // RING) * zz + 256 * cc + 88 * part + offsets[k]
+            dst = 24 * offsets[k] + r * group
+            pltpu.make_async_copy(tok_ref.at[pl.ds(src, r), :], xt.at[pl.ds(dst, r), :], xsem.at[k]).start()
+
     with jax.named_scope("prep_1"):
-        lax.fori_loop(3, 6, prep, 0)
+        lax.fori_loop(2, 5, prep, 0)
     with jax.named_scope("count_step_0"):
         count_step(0)
     with jax.named_scope("prep_2"):
-        lax.fori_loop(6, 8, prep, 0)
+        lax.fori_loop(5, 8, prep, 0)
     with jax.named_scope("count_step_1"):
         count_step(1)
     with jax.named_scope("count_last"):
@@ -163,20 +168,19 @@
         return carry
 
     with jax.named_scope("spread"):
-        lax.fori_loop(0, tok_rows // RS, spread_rows, 0, unroll=4)
-
-    def grad_quarter(q):
-        for row in range(0, tok_rows, RS):
-            gain = acol[row : row + RS, :]
-            less = drop[row : row + RS, :]
-            chosen = icol[row : row + RS, :]
-            for j in range(RING * q, RING * q + RING):
-                value = ptab[row : row + RS, j * LANES : (j + 1) * LANES] * (aux_ref[j : j + 1, :] - less)
-                value = jnp.where(chosen == lane_of(j), value + gain, value)
-                big = value.astype(jnp.bfloat16)
-                cols = slice((j - RING * q) * LANES, (j - RING * q + 1) * LANES)
-                gmat[q][0, row : row + RS, cols] = big
-                gmat[q][1, row : row + RS, cols] = (value - big.astype(jnp.float32)).astype(jnp.bfloat16)
+        lax.fori_loop(0, tok_rows // RS, spread_rows, 0, unroll=8)
+
+    def grad_piece(q, row):
+        gain = acol[row : row + RS, :]
+        less = drop[row : row + RS, :]
+        chosen = icol[row : row + RS, :]
+        for j in range(RING * q, RING * q + RING):
+            value = ptab[row : row + RS, j * LANES : (j + 1) * LANES] * (aux_ref[j : j + 1, :] - less)
+            value = jnp.where(chosen == lane_of(j), value + gain, value)
+            big = value.astype(jnp.bfloat16)
+            cols = slice((j - RING * q) * LANES, (j - RING * q + 1) * LANES)
+            gmat[q][0, row : row + RS, cols] = big
+            gmat[q][1, row : row + RS, cols] = (value - big.astype(jnp.float32)).astype(jnp.bfloat16)
 
     def pair_copy(k, first, count):
         rows = 12 * ROW_CHUNKS[k]
@@ -184,7 +188,9 @@
         return pltpu.make_async_remote_copy(
             src, drecv[k].at[pl.ds(first, count)], dsend.at[k], drsem.at[k], device_id=sibling, device_id_type=MESH)
 
-    def matmul_quarter(k, q):
+    NT, KT = 256, 256
+
+    def matmul_quarter(k, q, beside=()):
         rows = 24 * ROW_CHUNKS[k]
         base = 24 * offsets[k]
         if q == 0:
@@ -192,11 +198,23 @@
                 pair_copy(k - 2, 0, eblocks).wait_send()
             chunk_rows = xt.at[pl.ds(base, rows), :]
             pltpu.make_async_copy(chunk_rows, chunk_rows, xsem.at[k]).wait()
-        left = xt[base : base + rows, :]
-        value = jnp.dot(left, gmat[q][0], preferred_element_type=jnp.float32)
-        value = value + jnp.dot(left, gmat[q][1], preferred_element_type=jnp.float32)
-        for j in range(RING):
-            cbuf[k % 2, RING * q + j, 0:rows, :] = value[:, j * LANES : (j + 1) * LANES]
+        count = experts // RING // NT * 2 * (tok_rows // KT)
+        beside = list(beside)
+        each = -(-len(beside) // count)
+        for n in range(experts // RING // NT):
+            value = None
+            for half in range(2):
+                for kt in range(tok_rows // KT):
+                    part = jnp.dot(
+                        xt[base : base + rows, kt * KT : (kt + 1) * KT],
+                        gmat[q][half, kt * KT : (kt + 1) * KT, n * NT : (n + 1) * NT],
+                        preferred_element_type=jnp.float32)
+                    value = part if value is None else value + part
+                    for piece in beside[:each]:
+                        piece()
+                    beside = beside[each:]
+            for j in range(NT // LANES):
+                cbuf[k % 2, RING * q + n * (NT // LANES) + j, 0:rows, :] = value[:, j * LANES : (j + 1) * LANES]
         pair_copy(k, RING * q, RING).start()
 
     orders = ("xyz", "yzx", "zxy")
@@ -218,6 +236,8 @@
             (s.at[down, 0:2], f.at[1, 0:2], 2, left),
             (s.at[up, 0:2], f.at[0, 0:2], 2, right),
             (s.at[down, 2:4], f.at[1, 2:4], 2, left),
+            (s.at[up], f.at[0], 2, right),
+            (s.at[down], f.at[1], 2, left),
         )
         copies = []
         for n in numbers:
@@ -240,7 +260,8 @@
         i = pos(p, stage)
         up, down = (i + 1) % RING, (i + 3) % RING
         s, m = (sums, tmid)[stage][k], (r1m, r2m)[stage][k]
-        first, second, third, fourth = around(k, p, stage, (0, 1, 4, 5))
+        early = stage == 0 and k < EARLY_OWN
+        first, second, third, fourth = around(k, p, stage, (0, 1, 4, 5) if early else (0, 1, 6, 7))
         first.wait_recv()
         s[p, up, 0:2] = s[p, up, 0:2] + m[p, 0]
         third.start()
@@ -264,7 +285,7 @@
             return carry
 
         lax.fori_loop(0, eblocks, block, 0)
-        for n in range(4):
+        for n in range(4 if k < EARLY_OWN else 2):
             for p in range(3):
                 around(k, p, 0, (n,))[0].start()
 
@@ -276,7 +297,7 @@
         for p in range(3):
             taken(r1f[k].at[p], rsem.at[k, p, 2])
             tmid[k][p] = sums[k][p, pos(p, 0)] + r1f[k][p, 0] + r1f[k][p, 1]
-            for copy in around(k, p, 1, (0, 1, 2, 3)):
+            for copy in around(k, p, 1, (0, 1)):
                 copy.start()
 
     def stage_d(k):
@@ -299,22 +320,71 @@
             fin[row : row + r, :] = umid[k][p, pos(p, 2)] + r3[k][p, 0] + r3[k][p, 1] + r3[k][p, 2]
         taken(tmid[k].at[:, 0:3], ssem.at[k, 1])
 
-    plan = []
-    for k in range(chunks):
+    def plane_ring(k, p):
+        (one, i), (two, j) = (orders[p][1], pos(p, 1)), (orders[p][2], pos(p, 2))
+        copies = []
+        for n in range(1, RING * RING):
+            b, c = (i + n // RING) % RING, (j + n % RING) % RING
+            copies.append(pltpu.make_async_remote_copy(
+                tmid[k].at[p, b, c], plane[k].at[p, n - 1], ssem.at[k, 2], rsem.at[k, p, 6], device_id=device(**{one: b, two: c}), device_id_type=MESH))
+        return copies
+
+    def stage_plane(k):
+        for p in range(3):
+            taken(r1f[k].at[p], rsem.at[k, p, 2])
+            tmid[k][p] = sums[k][p, pos(p, 0)] + r1f[k][p, 0] + r1f[k][p, 1]
+            for copy in plane_ring(k, p):
+                copy.start()
+        taken(sums[k].at[:, 0:3], ssem.at[k, 0])
+
+    def stage_g(k):
+        r = ROW_CHUNKS[k]
+        for p in range(3):
+            taken(plane[k].at[p], rsem.at[k, p, 6])
+            row = 88 * p + offsets[k]
+            value = tmid[k][p, pos(p, 1), pos(p, 2)]
+            for n in range(RING * RING - 1):
+                value = value + plane[k][p, n]
+            fin[row : row + r, :] = value
+
+    def grad_pieces(q):
+        return [functools.partial(grad_piece, q, row) for row in range(0, tok_rows, RS)]
+
+    with jax.named_scope("first_chunk"):
+        for piece in grad_pieces(0):
+            piece()
         for q in range(RING):
-            plan.append((RING * k + q, -1, k, "matmul", functools.partial(matmul_quarter, k, q)))
-        for order, (stage, lag) in enumerate(((stage_a, 2), (stage_b, 5), (stage_c, 9), (stage_d, 12), (stage_e, 15), (stage_f, 18))):
-            plan.append((RING * k + 3 + lag, order, k, stage.__name__, functools.partial(stage, k)))
-    with jax.named_scope("first_chunk"):
-        for q in range(RING):
-            grad_quarter(q)
-            if q:
-                matmul_quarter(0, q - 1)
-        matmul_quarter(0, RING - 1)
-    for when, order, k, name, step in sorted(plan, key=lambda entry: entry[:3]):
-        if when >= RING:
-            with jax.named_scope(f"{name}_{k}"):
-                step()
+            matmul_quarter(0, q, grad_pieces(q + 1) if q + 1 < RING else ())
+
+    ring_stages = ((stage_a, 0.0), (stage_b, 0.088), (stage_c, 0.022), (stage_d, 0.044), (stage_e, 0.033), (stage_f, 0.0))
+    plane_stages = ((stage_a, 0.0), (stage_b, 0.088), (stage_plane, 0.175), (stage_g, 0.0))
+    quarters = [(k, q) for k in range(1, chunks) for q in range(RING)]
+    ready = [(PAIR_TIME, 0, 0)]
+    clock, links = 0.0, 0.0
+    while quarters or ready:
+        ready.sort()
+        if ready and (ready[0][0] <= clock or not quarters):
+            when, k, number = ready.pop(0)
+            stages = plane_stages if k in PLANE else ring_stages
+            stage, wire = stages[number]
+            r = ROW_CHUNKS[k]
+            clock = max(clock, when) + (0.04 if number else 0.025 * r)
+            with jax.named_scope(f"{stage.__name__}_{k}"):
+                stage(k)
+            if number == 0:
+                arrival = max(clock, links) + 0.088 * r
+                links = arrival + (0.088 * r if k < EARLY_OWN else 0.0)
+            else:
+                arrival = links = max(clock, links) + wire * r * (1 if number > 1 or k < EARLY_OWN else 2)
+            if number + 1 < len(stages):
+                ready.append((arrival + HOP_TIME + (1.5 if stage is stage_plane else 0.0), k, number + 1))
+        else:
+            k, q = quarters.pop(0)
+            with jax.named_scope(f"matmul_{k}"):
+                matmul_quarter(k, q)
+            clock += QUARTER_TIME * ROW_CHUNKS[k]
+            if q == RING - 1:
+                ready.append((clock + PAIR_TIME, k, 0))
 
     keep = keep_ref[pl.ds(ex, 1), :].astype(jnp.float32)
     rows = d_model // 8
@@ -328,7 +398,7 @@
     for k in range(max(chunks - 2, 0), chunks):
         pair_copy(k, 0, eblocks).wait_send()
     for k in range(chunks):
-        taken(umid[k].at[:, 0:3], ssem.at[k, 2])
+        taken(plane[k] if k in PLANE else umid[k].at[:, 0:3], ssem.at[k, 2])
 
 
 def solution(mesh):
@@ -347,7 +417,7 @@
             return [vm(shape_of(r), f32) for r in ROW_CHUNKS]
 
         scratch = [
-            vm((2, TB, experts), bf16),
+            vm((SLOTS, TB, experts), bf16),
             vm((tok_rows, LANES), i32),
             vm((tok_rows, LANES), f32),
             vm((tok_rows, LANES), f32),
@@ -364,11 +434,12 @@
             per_chunk(lambda r: (3, 2, 4, r, LANES)),
             per_chunk(lambda r: (3, 4, r, LANES)),
             per_chunk(lambda r: (3, 3, r, LANES)),
+            [vm((3, RING * RING - 1, r if k in PLANE else 8, LANES), f32) for k, r in enumerate(ROW_CHUNKS)],
             vm((264, LANES), f32),
             vm((3, eblocks, LANES), i32),
             vm((13, eblocks, LANES), i32),
             vm((eblocks, LANES), f32),
-            pltpu.SemaphoreType.DMA((2,)),
+            pltpu.SemaphoreType.DMA((SLOTS,)),
             pltpu.SemaphoreType.DMA((chunks,)),
             pltpu.SemaphoreType.DMA((3,)),
             pltpu.SemaphoreType.DMA((13,)),

time: 84 us -> 73.8 us (0.88)
  Pallas kernels: 82.1 us -> 72 us
    pallas_call x1, Pallas kernels: 82.1 us -> 72 us  [local(): pl.pallas_call(functools.partial(kernel, tok_rows * devices), out_shape=j...]
where the time goes in v4:
time: 73.8 us; the launch traced here: 73.6 us
  Pallas kernels  72 us (98%)
  local copies, waits for them, and re-layouts  1.57 us (2%)
    pallas_call x1, Pallas kernels, local(): pl.pallas_call(functools.partial(kernel, tok_rows * devices), out_shape=j...  72 us
    unnamed x1, local copies, waits for them, and re-layouts  1.57 us

profile of v4, /device:TPU:0, one launch (start us, length us, event | category | flops | bytes accessed | tf_op | source)
XLA Modules:
  0.0 73.6 jit_solution(4572475103623555881)
XLA Ops:
  0.0 72.0 %shard_map.55 = f32[260,128]{1,0:T(8,128)} custom-call(s32[8,128]{1,0:T(8,128)} %bitcast.8, f32[8,128]{1,0:T(8,128)} %bitcast.9, s32[16,128]{1,0:T(8,128)} %bitcast.7, bf16[2080,1024]{1,0:T(8,128)(2,1)} %bitcast.5, bf16[1024,2048]{1,0:T(8,128)(2,1)} %logit_ref.1), custom_call_target="tpu_custom_call" | custom-call | tf_op jit(solution)/shard_map/pallas_call | solution.py:451
  72.0 1.6 %copy.7 = f32[128,260]{0,1:T(8,128)} copy(f32[128,260]{0,1:T(8,128)} %bitcast.6) | data formatting | bytes 266240

commit v5 on v4

--- a/solution.py
+++ b/solution.py
@@ -9,7 +9,8 @@
 
 MESH = pl.DeviceIdType.MESH
 RING = 4
-PAIR_TIME, HOP_TIME, QUARTER_TIME = 1.5, 2.4, 0.0606
+LOW = jnp.float8_e5m2
+PAIR_TIME, HOP_TIME, QUARTER_TIME = 1.1, 2.4, 0.046
 PLANE = (5, 6)
 EARLY_OWN = 6
 LANES = 128
@@ -19,7 +20,7 @@
 
 
 def kernel(total_tokens, idx_ref, gate_ref, keep_ref, tok_ref, logit_ref, out_ref,
-           lbuf, icol, acol, drop, ptab, gmat, xt, cbuf, drecv, sums, r1m, r1f, tmid, r2m, r2f, umid, r3, plane,
+           lbuf, icol, acol, drop, ptab, gmat, glow, xt, xlow, cbuf, drecv, sums, r1m, r1f, tmid, r2m, r2f, umid, r3, plane,
            fin, cnt, cnt_recv, aux_ref,
            lsem, xsem, csend, crecv, dsend, drsem, ssem, rsem):
     d_model, tok_rows = tok_ref.shape
@@ -156,15 +157,31 @@
         lax.fori_loop(5, 8, prep, 0)
     with jax.named_scope("count_step_1"):
         count_step(1)
+    def lower_rows(n, carry):
+        at = pl.ds(pl.multiple_of(n * LR, LR), LR)
+        xlow[at, :] = xt[at, :].astype(LOW)
+        return carry
+
+    LR = 96
+    with jax.named_scope("lower"):
+        for k in range(chunks):
+            chunk_rows = xt.at[pl.ds(24 * offsets[k], 24 * ROW_CHUNKS[k]), :]
+            pltpu.make_async_copy(chunk_rows, chunk_rows, xsem.at[k]).wait()
+        lax.fori_loop(0, 24 * sum(ROW_CHUNKS) // LR, lower_rows, 0)
+
     with jax.named_scope("count_last"):
-        aux_ref[...] = count_arrive(2).astype(jnp.float32) * (experts / total_tokens)
+        raw = count_arrive(2).astype(jnp.float32) * (experts / total_tokens)
+        scale = 4194304.0 / (jnp.max(jnp.max(raw, axis=1, keepdims=True), axis=0, keepdims=True) + 6.0)
+        aux_ref[...] = raw * scale
 
     def spread_rows(r, carry):
         at = pl.ds(pl.multiple_of(r * RS, RS), RS)
         acc = ptab[at, 0:LANES] * aux_ref[0:1, :]
         for j in range(1, eblocks):
             acc = acc + ptab[at, j * LANES : (j + 1) * LANES] * aux_ref[j : j + 1, :]
-        drop[at, :] = jnp.sum(acc, axis=1, keepdims=True) + acol[at, :]
+        gain = acol[at, :] * scale
+        acol[at, :] = gain
+        drop[at, :] = jnp.sum(acc, axis=1, keepdims=True) + gain
         return carry
 
     with jax.named_scope("spread"):
@@ -178,9 +195,8 @@
             value = ptab[row : row + RS, j * LANES : (j + 1) * LANES] * (aux_ref[j : j + 1, :] - less)
             value = jnp.where(chosen == lane_of(j), value + gain, value)
             big = value.astype(jnp.bfloat16)
-            cols = slice((j - RING * q) * LANES, (j - RING * q + 1) * LANES)
-            gmat[q][0, row : row + RS, cols] = big
-            gmat[q][1, row : row + RS, cols] = (value - big.astype(jnp.float32)).astype(jnp.bfloat16)
+            gmat[q][j - RING * q, row : row + RS, :] = big
+            glow[q][j - RING * q, row : row + RS, :] = (value - big.astype(jnp.float32)).astype(LOW)
 
     def pair_copy(k, first, count):
         rows = 12 * ROW_CHUNKS[k]
@@ -196,8 +212,6 @@
         if q == 0:
             if k >= 2:
                 pair_copy(k - 2, 0, eblocks).wait_send()
-            chunk_rows = xt.at[pl.ds(base, rows), :]
-            pltpu.make_async_copy(chunk_rows, chunk_rows, xsem.at[k]).wait()
         count = experts // RING // NT * 2 * (tok_rows // KT)
         beside = list(beside)
         each = -(-len(beside) // count)
@@ -205,10 +219,10 @@
             value = None
             for half in range(2):
                 for kt in range(tok_rows // KT):
+                    left, right = ((xt, gmat), (xlow, glow))[half]
+                    right = [right[q][n * (NT // LANES) + j, kt * KT : (kt + 1) * KT, :] for j in range(NT // LANES)]
                     part = jnp.dot(
-                        xt[base : base + rows, kt * KT : (kt + 1) * KT],
-                        gmat[q][half, kt * KT : (kt + 1) * KT, n * NT : (n + 1) * NT],
-                        preferred_element_type=jnp.float32)
+                        left[base : base + rows, kt * KT : (kt + 1) * KT], jnp.concatenate(right, axis=1), preferred_element_type=jnp.float32)
                     value = part if value is None else value + part
                     for piece in beside[:each]:
                         piece()
@@ -388,7 +402,7 @@
 
     keep = keep_ref[pl.ds(ex, 1), :].astype(jnp.float32)
     rows = d_model // 8
-    whole = fin[...] * keep
+    whole = fin[...] * (keep / scale)
     first, second = whole[0:rows, :], whole[whole.shape[0] - rows :, :]
     out_ref[...] = jnp.where(core == 0, first, second)
 
@@ -422,8 +436,10 @@
             vm((tok_rows, LANES), f32),
             vm((tok_rows, LANES), f32),
             vm((tok_rows, experts), f32),
-            [vm((2, tok_rows, experts // RING), bf16)] * RING,
+            [vm((RING, tok_rows, LANES), bf16)] * RING,
+            [vm((RING, tok_rows, LANES), LOW)] * RING,
             vm((24 * sum(ROW_CHUNKS), tok_rows), bf16),
+            vm((24 * sum(ROW_CHUNKS), tok_rows), LOW),
             vm((2, eblocks, 24 * rmax, LANES), f32),
             per_chunk(lambda r: (eblocks, 12 * r, LANES)),
             per_chunk(lambda r: (3, 4, 4, 4, r, LANES)),

time: 73.8 us -> 71.2 us (0.965)
  Pallas kernels: 72 us -> 69.4 us
    pallas_call x1, Pallas kernels: 72 us -> 69.4 us  [local(): pl.pallas_call(functools.partial(kernel, tok_rows * devices), out_shape=j...]
where the time goes in v5:
time: 71.2 us; the launch traced here: 71 us
  Pallas kernels  69.4 us (97%)
  local copies, waits for them, and re-layouts  1.57 us (2%)
    pallas_call x1, Pallas kernels, local(): pl.pallas_call(functools.partial(kernel, tok_rows * devices), out_shape=j...  69.4 us
    unnamed x1, local copies, waits for them, and re-layouts  1.57 us

profile of v5, /device:TPU:0, one launch (start us, length us, event | category | flops | bytes accessed | tf_op | source)
XLA Modules:
  0.0 71.0 jit_solution(7340705822780604124)
XLA Ops:
  0.0 69.4 %shard_map.55 = f32[260,128]{1,0:T(8,128)} custom-call(s32[8,128]{1,0:T(8,128)} %bitcast.8, f32[8,128]{1,0:T(8,128)} %bitcast.9, s32[16,128]{1,0:T(8,128)} %bitcast.7, bf16[2080,1024]{1,0:T(8,128)(2,1)} %bitcast.5, bf16[1024,2048]{1,0:T(8,128)(2,1)} %logit_ref.1), custom_call_target="tpu_custom_call" | custom-call | tf_op jit(solution)/shard_map/pallas_call | solution.py:467
  69.4 1.6 %copy.7 = f32[128,260]{0,1:T(8,128)} copy(f32[128,260]{0,1:T(8,128)} %bitcast.6) | data formatting | bytes 266240

commit v6 on v5

--- a/solution.py
+++ b/solution.py
@@ -11,10 +11,10 @@
 RING = 4
 LOW = jnp.float8_e5m2
 PAIR_TIME, HOP_TIME, QUARTER_TIME = 1.1, 2.4, 0.046
-PLANE = (5, 6)
+PLANE = (6,)
 EARLY_OWN = 6
 LANES = 128
-ROW_CHUNKS = (8, 8, 16, 16, 16, 16, 8)
+ROW_CHUNKS = (8, 16, 16, 16, 16, 8, 8)
 TB = 128
 SLOTS = 3
 

time: 71.2 us -> 70.4 us (0.989)
  Pallas kernels: 69.4 us -> 68.6 us
    pallas_call x1, Pallas kernels: 69.4 us -> 68.6 us  [local(): pl.pallas_call(functools.partial(kernel, tok_rows * devices), out_shape=j...]
where the time goes in v6:
time: 70.4 us; the launch traced here: 70.2 us
  Pallas kernels  68.6 us (97%)
  local copies, waits for them, and re-layouts  1.57 us (2%)
    pallas_call x1, Pallas kernels, local(): pl.pallas_call(functools.partial(kernel, tok_rows * devices), out_shape=j...  68.6 us
    unnamed x1, local copies, waits for them, and re-layouts  1.57 us

profile of v6, /device:TPU:0, one launch (start us, length us, event | category | flops | bytes accessed | tf_op | source)
XLA Modules:
  0.0 70.2 jit_solution(3272034941562453953)
XLA Ops:
  0.0 68.6 %shard_map.55 = f32[260,128]{1,0:T(8,128)} custom-call(s32[8,128]{1,0:T(8,128)} %bitcast.8, f32[8,128]{1,0:T(8,128)} %bitcast.9, s32[16,128]{1,0:T(8,128)} %bitcast.7, bf16[2080,1024]{1,0:T(8,128)(2,1)} %bitcast.5, bf16[1024,2048]{1,0:T(8,128)(2,1)} %logit_ref.1), custom_call_target="tpu_custom_call" | custom-call | tf_op jit(solution)/shard_map/pallas_call | solution.py:467
  68.6 1.6 %copy.7 = f32[128,260]{0,1:T(8,128)} copy(f32[128,260]{0,1:T(8,128)} %bitcast.6) | data formatting | bytes 266240

commit v7 on v6

--- a/solution.py
+++ b/solution.py
@@ -154,9 +154,11 @@
     with jax.named_scope("count_step_0"):
         count_step(0)
     with jax.named_scope("prep_2"):
-        lax.fori_loop(5, 8, prep, 0)
+        lax.fori_loop(5, 7, prep, 0)
     with jax.named_scope("count_step_1"):
         count_step(1)
+    with jax.named_scope("prep_3"):
+        lax.fori_loop(7, 8, prep, 0)
     def lower_rows(n, carry):
         at = pl.ds(pl.multiple_of(n * LR, LR), LR)
         xlow[at, :] = xt[at, :].astype(LOW)

time: 70.4 us -> 70.4 us (level)
  no operation moved by 1% of the time
where the time goes in v7:
time: 70.4 us; the launch traced here: 70.2 us
  Pallas kernels  68.6 us (97%)
  local copies, waits for them, and re-layouts  1.57 us (2%)
    pallas_call x1, Pallas kernels, local(): pl.pallas_call(functools.partial(kernel, tok_rows * devices), out_shape=j...  68.6 us
    unnamed x1, local copies, waits for them, and re-layouts  1.57 us

profile of v7, /device:TPU:0, one launch (start us, length us, event | category | flops | bytes accessed | tf_op | source)
XLA Modules:
  0.0 70.2 jit_solution(5843740313823267302)
XLA Ops:
  0.0 68.6 %shard_map.55 = f32[260,128]{1,0:T(8,128)} custom-call(s32[8,128]{1,0:T(8,128)} %bitcast.8, f32[8,128]{1,0:T(8,128)} %bitcast.9, s32[16,128]{1,0:T(8,128)} %bitcast.7, bf16[2080,1024]{1,0:T(8,128)(2,1)} %bitcast.5, bf16[1024,2048]{1,0:T(8,128)(2,1)} %logit_ref.1), custom_call_target="tpu_custom_call" | custom-call | tf_op jit(solution)/shard_map/pallas_call | solution.py:469
  68.6 1.6 %copy.7 = f32[128,260]{0,1:T(8,128)} copy(f32[128,260]{0,1:T(8,128)} %bitcast.6) | data formatting | bytes 266240

commit v8 on v7

--- a/solution.py
+++ b/solution.py
@@ -135,7 +135,7 @@
         return carry
 
     with jax.named_scope("prep_0"):
-        lax.fori_loop(0, 2, prep, 0)
+        lax.fori_loop(0, 1, prep, 0)
     with jax.named_scope("barrier"):
         pl.semaphore_wait(barrier, len(peers))
     for copy in count_copies(0):
@@ -150,7 +150,7 @@
             pltpu.make_async_copy(tok_ref.at[pl.ds(src, r), :], xt.at[pl.ds(dst, r), :], xsem.at[k]).start()
 
     with jax.named_scope("prep_1"):
-        lax.fori_loop(2, 5, prep, 0)
+        lax.fori_loop(1, 5, prep, 0)
     with jax.named_scope("count_step_0"):
         count_step(0)
     with jax.named_scope("prep_2"):

time: 70.4 us -> 70.2 us (level)
  no operation moved by 1% of the time
where the time goes in v8:
time: 70.2 us; the launch traced here: 70 us
  Pallas kernels  68.4 us (97%)
  local copies, waits for them, and re-layouts  1.57 us (2%)
    pallas_call x1, Pallas kernels, local(): pl.pallas_call(functools.partial(kernel, tok_rows * devices), out_shape=j...  68.4 us
    unnamed x1, local copies, waits for them, and re-layouts  1.57 us

profile of v8, /device:TPU:0, one launch (start us, length us, event | category | flops | bytes accessed | tf_op | source)
XLA Modules:
  0.0 70.0 jit_solution(10782883604869032909)
XLA Ops:
  0.0 68.4 %shard_map.55 = f32[260,128]{1,0:T(8,128)} custom-call(s32[8,128]{1,0:T(8,128)} %bitcast.8, f32[8,128]{1,0:T(8,128)} %bitcast.9, s32[16,128]{1,0:T(8,128)} %bitcast.7, bf16[2080,1024]{1,0:T(8,128)(2,1)} %bitcast.5, bf16[1024,2048]{1,0:T(8,128)(2,1)} %logit_ref.1), custom_call_target="tpu_custom_call" | custom-call | tf_op jit(solution)/shard_map/pallas_call | solution.py:469
  68.4 1.6 %copy.7 = f32[128,260]{0,1:T(8,128)} copy(f32[128,260]{0,1:T(8,128)} %bitcast.6) | data formatting | bytes 266240
